TPU v7x, 32 devices: a whole 2x2x4 slice. The times are simulated.
32 devices in a mesh: reg: 4 (over y, core), prod: 8 (over z, x).
Axes of the slice: x: 2, y: 2, z: 4, core: 2. Of those that a mesh axis runs over, the one named last changes fastest.
Arguments:
- bottom_series_predictions: float32 [128, 256, 128], P('reg', 'prod'), may hold values from -6 to 6
- group_item_predictions: float32 [32, 256, 128], P('reg', 'prod'), may hold values from -18 to 18
- area_class_predictions: float32 [128, 32, 128], P('reg', 'prod'), may hold values from -18 to 18
- group_class_predictions: float32 [32, 32, 128], P('reg'), may hold values from -48 to 48
- bottom_series_precision: float32 [128, 256], P('reg', 'prod'), may hold values from 0.5 to 5
- group_item_precision: float32 [32, 256], P('reg', 'prod'), may hold values from 0.02 to 0.5
- area_class_precision: float32 [128, 32], P('reg', 'prod'), may hold values from 0.02 to 0.5
- group_class_precision: float32 [32, 32], P('reg'), may hold values from 0.002 to 0.05
- group_area_partition: int32 [32, 128], replicated, may hold values from -1 to 127, as said below
- class_item_partition: int32 [32, 128], replicated, may hold values from -1 to 255, as said below
Outputs:
- solution_field: float32 [128, 256, 128], P('reg', 'prod')
- residual: float32 [128, 256, 128], P('reg', 'prod')
Inputs may be any that keep to these rules, and one draw needn't show every extreme that they name: `group_area_partition`: every region stands in exactly one row; each row holds its parent's regions in its first slots and -1 in the rest; a parent has 1 to 97 regions, and some parent has exactly 97. `class_item_partition`: every product stands in exactly one row; each row holds its category's products in its first slots and -1 in the rest; a category has 1 to 128 products, and some category has exactly 128.
All inputs are finite; a program needn't handle non-finite values.
Results may differ from a plain program's by a relative error of at most 0.00011.
Values sent between devices are 32-bit elements; how exact they have to be, the bound alone decides.
A program may use at most 64 MiB of HBM per device.

v0:
```python
import jax
import jax.numpy as jnp
from jax import lax
from jax.sharding import PartitionSpec as P

ITERATIONS = 2


def member_local(table, first, count):
    items = first + jnp.arange(count, dtype=jnp.int32)
    return jnp.any(table[:, :, None] == items[None, None, :], axis=1).astype(jnp.float32)


def on_device(
    bottom_series_predictions,
    group_item_predictions,
    area_class_predictions,
    group_class_predictions,
    bottom_series_precision,
    group_item_precision,
    area_class_precision,
    group_class_precision,
    group_area_partition,
    class_item_partition,
):
    high = lax.Precision.HIGHEST
    areas_overall, items_overall, horizon_length = bottom_series_predictions.shape
    area_index_table = member_local(
        group_area_partition, lax.axis_index("reg") * areas_overall, areas_overall
    )
    item_index_table = member_local(
        class_item_partition, lax.axis_index("prod") * items_overall, items_overall
    )
    parent_share = area_index_table.shape[0] // lax.axis_size("reg")

    def disaggregate_onto(upper, lower):
        block = area_index_table
        total = jnp.einsum(
            "pr,pqh->rqh", block, lax.all_gather(upper, "reg", axis=0, tiled=True), precision=high
        )
        block = item_index_table
        return total + jnp.einsum(
            "crh,cq->rqh", lax.all_gather(lower, "prod", axis=0, tiled=True), block, precision=high
        )

    def replicate_across(corner):
        return jnp.einsum("pch,cq->pqh", corner, item_index_table, precision=high)

    def operate(field):
        rows_local = jnp.einsum("pr,rqh->pqh", area_index_table, field, precision=high)
        row_share = lax.psum_scatter(rows_local, "reg", scatter_dimension=0, tiled=True)
        col_share = lax.psum_scatter(
            jnp.einsum("cq,rqh->crh", item_index_table, field, precision=high),
            "prod",
            scatter_dimension=0,
            tiled=True,
        )
        partial_corner = jnp.einsum("pqh,cq->pch", rows_local, item_index_table, precision=high)
        whole = lax.psum(partial_corner, ("reg", "prod"))
        corner_share = lax.dynamic_slice_in_dim(
            whole, lax.axis_index("reg") * parent_share, parent_share, 0
        )
        upper = group_item_precision[:, :, None] * row_share + replicate_across(
            group_class_precision[:, :, None] * corner_share
        )
        lower = jnp.transpose(area_class_precision)[:, :, None] * col_share
        return bottom_series_precision[:, :, None] * field + disaggregate_onto(upper, lower)

    major_axis_first = group_item_precision[:, :, None] * group_item_predictions + replicate_across(
        group_class_precision[:, :, None] * group_class_predictions
    )
    lower_leading = jnp.transpose(
        area_class_precision[:, :, None] * area_class_predictions, (1, 0, 2)
    )
    system_source_term = bottom_series_precision[
        :, :, None
    ] * bottom_series_predictions + disaggregate_onto(major_axis_first, lower_leading)

    def two_products(vector, image):
        return lax.psum((jnp.sum(vector * vector), jnp.sum(vector * image)), ("reg", "prod"))

    solution_field = jnp.zeros_like(system_source_term)
    residual = system_source_term
    image = operate(residual)
    norm_now, product = two_products(residual, image)
    alpha = norm_now / product
    direction, along = (residual, image)
    for step in range(ITERATIONS):
        solution_field = solution_field + alpha * direction
        residual = residual - alpha * along
        if step + 1 < ITERATIONS:
            image = operate(residual)
            norm_next, product = two_products(residual, image)
            ratio = norm_next / norm_now
            alpha = norm_next / (product - ratio * norm_next / alpha)
            direction = residual + ratio * direction
            along = image + ratio * along
            norm_now = norm_next
    return (solution_field, residual)


def solution(mesh):
    return jax.shard_map(
        on_device,
        mesh=mesh,
        in_specs=(
            P("reg", "prod", None),
            P("reg", "prod", None),
            P("reg", "prod", None),
            P("reg", None, None),
            P("reg", "prod"),
            P("reg", "prod"),
            P("reg", "prod"),
            P("reg", None),
            P(),
            P(),
        ),
        out_specs=(P("reg", "prod", None), P("reg", "prod", None)),
        check_vma=False,
    )
```

profile of v0, /device:TPU:0, one launch (start us, length us, event | category | flops | bytes accessed | tf_op | source)
XLA Modules:
  0.0 496.6 jit_solution(14481580540045878076)
XLA Ops:
  10.1 1.3 fusion.5
  11.4 8.8 %all_gather.18 = f32[32,32,128]{2,1,0:T(8,128)S(1)} all-gather(f32[8,32,128]{2,1,0:T(8,128)S(1)} %fusion.5), channel_id=1, replica_groups=mesh['reg'=4,'prod'=8] {'reg'}, dimensions={0}, use_global_device_ids=true | all-gather | bytes 655360 | tf_op jit(solution)/shard_map/all_gather | solution.py:39
  20.3 31.9 %all_gather.19 = f32[32,32,128]{2,1,0:T(8,128)S(1)} all-gather(f32[4,32,128]{2,1,0:T(8,128)S(1)} %fusion.24), channel_id=1, replica_groups=mesh['reg'=4,'prod'=8] {'prod'}, dimensions={0}, use_global_device_ids=true | all-gather | bytes 589824 | tf_op jit(solution)/shard_map/all_gather | solution.py:43
  53.6 1.3 fusion.2
  55.3 1.5 convolution_bitcast_fusion.1
  56.9 1.1 copy.80
  58.8 1.1 copy.86
  59.9 126.6 %all-reduce.5.cloned.1.call-done = f32[32,32,128]{2,1,0:T(8,128)} async-done(((f32[32,32,128]{2,1,0:T(8,128)}), f32[32,32,128]{2,1,0:T(8,128)}) %all-reduce.5.cloned.1.call-update) | async-done | bytes 524304 | tf_op jit(solution)/shard_map/psum | solution.py:59
  186.6 1.3 fusion.4
  187.8 7.2 %all_gather.20 = f32[32,32,128]{2,1,0:T(8,128)S(1)} all-gather(f32[8,32,128]{2,1,0:T(8,128)S(1)} %fusion.4), channel_id=1, replica_groups=mesh['reg'=4,'prod'=8] {'reg'}, dimensions={0}, use_global_device_ids=true | all-gather | bytes 655360 | tf_op jit(solution)/shard_map/all_gather | solution.py:39
  195.9 31.4 %all_gather.21 = f32[32,32,128]{2,1,0:T(8,128)S(1)} all-gather(f32[4,32,128]{2,1,0:T(8,128)S(1)} %broadcast_multiply_fusion.1), channel_id=1, replica_groups=mesh['reg'=4,'prod'=8] {'prod'}, dimensions={0}, use_global_device_ids=true | all-gather | bytes 589824 | tf_op jit(solution)/shard_map/all_gather | solution.py:43
  228.0 1.6 multiply_reduce_fusion.2
  229.6 38.0 %all-reduce.1 = (f32[]{:T(128)}, f32[]{:T(128)}) all-reduce(f32[]{:T(128)} %get-tuple-element.13, f32[]{:T(128)} %get-tuple-element.12), channel_id=1, replica_groups=mesh['reg'=4,'prod'=8] {'reg','prod'}, use_global_device_ids=true, to_apply=%region_3.0 | all-reduce | flops 2 | bytes 16 | tf_op jit(solution)/shard_map/psum | solution.py:80
  269.4 1.5 convolution_bitcast_fusion
  271.0 1.1 copy.90
  273.0 1.1 copy.96
  274.2 126.9 %all-reduce.7.cloned.1.call-done = f32[32,32,128]{2,1,0:T(8,128)} async-done(((f32[32,32,128]{2,1,0:T(8,128)}), f32[32,32,128]{2,1,0:T(8,128)}) %all-reduce.7.cloned.1.call-update) | async-done | bytes 524304 | tf_op jit(solution)/shard_map/psum | solution.py:59
  401.0 1.3 fusion.3
  402.3 7.2 %all_gather.22 = f32[32,32,128]{2,1,0:T(8,128)S(1)} all-gather(f32[8,32,128]{2,1,0:T(8,128)S(1)} %fusion.3), channel_id=1, replica_groups=mesh['reg'=4,'prod'=8] {'reg'}, dimensions={0}, use_global_device_ids=true | all-gather | bytes 655360 | tf_op jit(solution)/shard_map/all_gather | solution.py:39
  410.4 31.4 %all_gather.23 = f32[32,32,128]{2,1,0:T(8,128)S(1)} all-gather(f32[4,32,128]{2,1,0:T(8,128)S(1)} %broadcast_multiply_fusion), channel_id=1, replica_groups=mesh['reg'=4,'prod'=8] {'prod'}, dimensions={0}, use_global_device_ids=true | all-gather | bytes 589824 | tf_op jit(solution)/shard_map/all_gather | solution.py:43
  442.5 1.6 multiply_reduce_fusion
  444.1 38.0 %all-reduce = (f32[]{:T(128)}, f32[]{:T(128)}) all-reduce(f32[]{:T(128)} %get-tuple-element.11, f32[]{:T(128)} %get-tuple-element.10), channel_id=1, replica_groups=mesh['reg'=4,'prod'=8] {'reg','prod'}, use_global_device_ids=true, to_apply=%region_10.0 | all-reduce | flops 2 | bytes 16 | tf_op jit(solution)/shard_map/psum | solution.py:80
  486.8 1.1 copy.101
  487.9 1.1 copy.100
  (49 shorter events, 9.9 us)
Async XLA Ops:
  8.0 0.7 copy-start.5
  8.0 178.6 %all-reduce.5.cloned.1.call-start = ((), (), s32[]{:S(2)}) async-start(), calls=%async_computation.5 | async-start | bytes 1048576 | tf_op jit(solution)/shard_map/psum | solution.py:59
  8.7 0.7 copy-start.6
  9.4 0.7 copy-start.2
  9.4 0.7 copy-start.3
  11.4 8.8 %copy-start.1 = (f32[32,4,128]{2,1,0:T(4,128)S(1)}, f32[32,4,128]{2,1,0:T(4,128)}, u32[]{:S(2)}) copy-start(f32[32,4,128]{2,1,0:T(4,128)} %param.12) | copy-start | bytes 196612
  11.4 8.8 %copy-start.4 = (f32[32,4]{0,1:T(4,128)S(1)}, f32[32,4]{0,1:T(4,128)}, u32[]{:S(2)}) copy-start(f32[32,4]{0,1:T(4,128)} %param.16) | copy-start | bytes 1540
  52.2 0.7 copy-start.7
  52.2 1.4 copy-start
  56.8 129.8 %reduce-scatter.5.cloned.1.call-start = ((), (), s32[]{:S(2)}) async-start(), calls=%async_computation.4 | async-start | bytes 655360 | tf_op jit(solution)/shard_map/reduce_scatter | solution.py:51
  58.0 137.0 %reduce-scatter.7.cloned.1.call-start = ((), (), s32[]{:S(2)}) async-start(), calls=%async_computation.6 | async-start | bytes 589824 | tf_op jit(solution)/shard_map/reduce_scatter | solution.py:52
  59.9 341.1 %all-reduce.7.cloned.1.call-start = ((), (), s32[]{:S(2)}) async-start(), calls=%async_computation.8 | async-start | bytes 1048576 | tf_op jit(solution)/shard_map/psum | solution.py:59
  270.9 130.1 %reduce-scatter.9.cloned.1.call-start = ((), (), s32[]{:S(2)}) async-start(), calls=%async_computation.7 | async-start | bytes 655360 | tf_op jit(solution)/shard_map/reduce_scatter | solution.py:51
  272.1 137.4 %reduce-scatter.11.cloned.1.call-start = ((), (), s32[]{:S(2)}) async-start(), calls=%async_computation.9 | async-start | bytes 589824 | tf_op jit(solution)/shard_map/reduce_scatter | solution.py:52
Sparse Core Ops, SparseCore 0:
  56.9 129.5 all-reduce.4
  271.0 129.9 all-reduce.6
Sparse Core Ops, SparseCore 1:
  59.8 21.9 reduce-scatter.4
  85.5 62.7 reduce-scatter.6
  273.9 22.3 reduce-scatter.8
  300.2 62.7 reduce-scatter.10
where the time goes:
time: 498 us; the launch traced here: 497 us
  waiting for transfers between devices  254 us (51%)
  blocking collectives  194 us (39%)
  between operations  21.7 us (4%)
  matrix products  15.5 us (3%)
  local copies, waits for them, and re-layouts  8.02 us (2%)
    psum x2, waiting for transfers between devices, operate(): whole = lax.psum(partial_corner, ('reg', 'prod'))  253 us
    all_gather x3, blocking collectives, disaggregate_onto(): lax.all_gather(lower, 'prod', axis=0, tiled=True)  94.6 us
    psum x2, blocking collectives, two_products(): lax.psum((jnp.sum(vector * vector), jnp.sum(vector * image)), ('reg', 'pr...  76 us
    all_gather x3, blocking collectives, disaggregate_onto(): lax.all_gather(upper, 'reg', axis=0, tiled=True)  23.1 us
  transfers between devices with their start and end apart: 6, of which 2 were waited for; matrix products, arithmetic and copies ran while one was open for 2% of the time, Pallas kernels for 0%

commit v1 on v0

v1 whole, which is shorter than its diff:
```python
import functools

import jax
import jax.numpy as jnp
from jax import lax
from jax.experimental import pallas as pl
from jax.experimental.pallas import tpu as pltpu
from jax.sharding import PartitionSpec as P

MESH = pl.DeviceIdType.MESH
ITERATIONS = 2
LANES = 128


def halves(x):
    hi = x.astype(jnp.bfloat16)
    lo = (x - hi.astype(jnp.float32)).astype(jnp.bfloat16)
    return jnp.concatenate([hi, lo], axis=0)


def apply_map(map2, x):
    return jnp.dot(map2, halves(x), preferred_element_type=jnp.float32)


def kernel(
    nr, np_, shared, per_tile,
    par_ref, kidx_ref, mask_ref,
    b_ref, dt_ref, u_ref, z_ref, v_ref, wt_ref, at_ref, rs_ref, p2_ref, pt2_ref, e2_ref,
    x_ref, res_ref,
    wt_buf, at_buf, uz_buf, g0_buf, uz_send,
    db, wcol, wgi, wgc, r0_buf, img0, img1,
    col_send, rs_buf, own, vbuf, gbuf, row_send, row_buf, rows_w, cor_send, cor_buf, zed,
    sc_send, sc_buf, sd_send, sd_buf,
    s_w, r_w, s_uz, r_uz, s_a, r_a, s_v, r_v,
    s_rs, r_rs, s_ag, r_ag, s_row, r_row, s_cor, r_cor, s_sc, r_sc, s_sd, r_sd,
):
    regions, items, horizon = b_ref.shape
    classes = p2_ref.shape[0]
    slab = regions // np_
    gs = u_ref.shape[0]
    mr = lax.axis_index("reg")
    mp = lax.axis_index("prod")

    def to(axis, me, n, s):
        return {axis: lax.rem(me + s, n)}

    def reg_copy(src, dst, ss, rr, s):
        return pltpu.make_async_remote_copy(
            src_ref=src, dst_ref=dst, send_sem=ss, recv_sem=rr,
            device_id=to("reg", mr, nr, s), device_id_type=MESH)

    def prod_copy(src, dst, ss, rr, s):
        return pltpu.make_async_remote_copy(
            src_ref=src, dst_ref=dst, send_sem=ss, recv_sem=rr,
            device_id=to("prod", mp, np_, s), device_id_type=MESH)

    barrier = pltpu.get_barrier_semaphore()
    for s in range(1, nr):
        pl.semaphore_signal(barrier, inc=1, device_id=to("reg", mr, nr, s), device_id_type=MESH)

    def greet(s, c):
        pl.semaphore_signal(barrier, inc=1, device_id=to("prod", mp, np_, s), device_id_type=MESH)
        return c

    lax.fori_loop(1, np_, greet, 0)
    for g in range(gs):
        uz_send[g] = u_ref[g] + apply_map(pt2_ref[...], z_ref[g])
    pl.semaphore_wait(barrier, nr - 1 + np_ - 1)

    def each_prod(f):
        lax.fori_loop(1, np_, lambda s, c: (f(s), c)[1], 0)

    def w_copy(s):
        return reg_copy(wt_ref, wt_buf.at[s], s_w.at[s], r_w.at[s], s)

    def uz_copy(s):
        return reg_copy(uz_send, uz_buf.at[pl.ds(mr * gs, gs)], s_uz.at[s], r_uz.at[s], s)

    def a_copy(s):
        return prod_copy(at_ref, at_buf.at[mp], s_a.at[s], r_a.at[s], s)

    def v_copy(s):
        return prod_copy(v_ref, g0_buf.at[mp], s_v.at[s], r_v.at[s], s)

    for s in range(1, nr):
        w_copy(s).start()
    each_prod(lambda s: v_copy(s).start())
    for s in range(1, nr):
        uz_copy(s).start()
    each_prod(lambda s: a_copy(s).start())
    g0_buf[mp] = v_ref[...]
    at_buf[mp] = at_ref[...]
    for g in range(gs):
        uz_buf[mr * gs + g] = uz_send[g]
    base = dt_ref[...]
    for r in range(regions):
        r0_buf[r] = jnp.broadcast_to(base[:, r : r + 1], (items, horizon)) * b_ref[r]
    total = wt_ref[...]
    for s in range(1, nr):
        w_copy(s).wait_recv()
        total = total + wt_buf[s]
    weights = jnp.dot(total, rs_ref[...], precision=lax.Precision.HIGHEST, preferred_element_type=jnp.float32)
    diag = base + weights[:items]
    for r in range(regions):
        db[r] = jnp.broadcast_to(diag[:, r : r + 1], (items, horizon))
    for k in range(shared):
        wgi[k] = jnp.broadcast_to(weights[:items, regions + k : regions + k + 1], (items, horizon))
        wgc[k] = jnp.broadcast_to(weights[items:, regions + k : regions + k + 1], (classes, horizon))

    each_prod(lambda s: a_copy(s).wait_recv())
    tiles = []
    for first in range(0, np_, per_tile):
        tile = at_buf[first]
        for j in range(first + 1, first + per_tile):
            tile = tile + at_buf[j]
        tiles.append(tile)
    wac = jnp.concatenate(tiles, axis=0) + weights[items:]
    lane = lax.broadcasted_iota(jnp.int32, (classes, LANES), 1)
    for i in range(slab):
        column = jnp.sum(jnp.where(lane == mp * slab + i, wac, 0.0), axis=1, keepdims=True)
        wcol[i] = jnp.broadcast_to(column, (classes, horizon))

    for s in range(1, nr):
        uz_copy(s).wait_recv()
    each_prod(lambda s: v_copy(s).wait_recv())

    def first_field(a, c):
        flat = jnp.concatenate([g0_buf[j, a] for j in range(np_)], axis=0)
        lifted = apply_map(e2_ref[...], flat)
        for t in range(per_tile):
            r = a * per_tile + t
            r0_buf[r] = r0_buf[r] + uz_buf[par_ref[r]] + lifted[t * items : (t + 1) * items]
        return c

    lax.fori_loop(0, regions // per_tile, first_field, 0)

    row_id = lax.broadcasted_iota(jnp.int32, (8, horizon), 0)
    norm_was = alpha_was = None
    for op in range(ITERATIONS):
        field = r0_buf if op == 0 else res_ref
        image = img0 if op == 0 else img1

        def row_copy(s, op=op):
            return reg_copy(row_send.at[op], row_buf.at[op, s], s_row.at[op, s], r_row.at[op, s], s)

        def rs_copy(s, op=op):
            return prod_copy(col_send.at[op, s], rs_buf.at[op, s], s_rs.at[op, s], r_rs.at[op, s], s)

        def cor_copy(s, op=op):
            return prod_copy(cor_send.at[op], cor_buf.at[op, s], s_cor.at[op, s], r_cor.at[op, s], s)

        def ag_copy(s, op=op):
            return prod_copy(vbuf.at[op], gbuf.at[op, pl.ds(mp * slab, slab)], s_ag.at[op, s], r_ag.at[op, s], s)

        def sc_copy(s, op=op):
            return reg_copy(sc_send.at[op], sc_buf.at[op, s], s_sc.at[op, s], r_sc.at[op, s], s)

        def sd_copy(s, op=op):
            return prod_copy(sd_send.at[op], sd_buf.at[op, s], s_sd.at[op, s], r_sd.at[op, s], s)

        def one_row(k, c, op=op, field=field):
            def add(r, acc):
                return acc + jnp.where(kidx_ref[r] == k, mask_ref[r], 0.0) * field[r]

            row_send[op, k] = lax.fori_loop(0, regions, add, jnp.zeros((items, horizon), jnp.float32))
            return c

        lax.fori_loop(0, shared, one_row, 0)
        for s in range(1, nr):
            row_copy(s).start()

        def columns(s, op=op, field=field):
            first = lax.rem(mp + s, np_) * slab
            wide = jnp.concatenate([field[first + i] for i in range(slab)], axis=1)
            out = apply_map(p2_ref[...], wide)
            return [out[:, i * horizon : (i + 1) * horizon] for i in range(slab)]

        def send_columns(s, op=op):
            for i, one in enumerate(columns(s)):
                col_send[op, s, i] = one
            rs_copy(s).start()

        each_prod(send_columns)
        for i, one in enumerate(columns(0)):
            own[i] = one

        for s in range(1, nr):
            row_copy(s).wait_recv()

        def one_corner(k, acc, op=op):
            rows = row_send[op, k]
            for s in range(1, nr):
                rows = rows + row_buf[op, s, k]
            weighted = wgi[k] * rows
            rows_w[k] = weighted
            cor_send[op, k] = apply_map(p2_ref[...], rows)
            return acc + weighted * rows

        row_part = lax.fori_loop(0, shared, one_corner, jnp.zeros((items, horizon), jnp.float32))
        each_prod(lambda s: cor_copy(s).start())

        def diagonal(r, acc, field=field, image=image):
            v = field[r]
            w = db[r] * v
            image[r] = w
            return acc[0] + v * v, acc[1] + w * v

        zero = jnp.zeros((items, horizon), jnp.float32)
        norm_part, along_part = lax.fori_loop(0, regions, diagonal, (zero, zero))
        along_part = along_part + row_part * (1.0 / nr)

        each_prod(lambda s: cor_copy(s).wait_recv())

        def one_zed(k, acc, op=op):
            corner = lax.fori_loop(1, np_, lambda s, c: c + cor_buf[op, s, k], cor_send[op, k])
            weighted = wgc[k] * corner
            zed[k] = weighted
            return acc + weighted * corner

        czero = jnp.zeros((classes, horizon), jnp.float32)
        cor_part = lax.fori_loop(0, shared, one_zed, czero) * (1.0 / (nr * np_))

        each_prod(lambda s: rs_copy(s).wait_recv())
        for i in range(slab):
            r = mp * slab + i
            cols = lax.fori_loop(1, np_, lambda s, c, i=i, op=op: c + rs_buf[op, s, i], own[i])
            weighted = wcol[i] * cols
            cor_part = cor_part + weighted * cols
            value = weighted + mask_ref[r] * zed[kidx_ref[r]]
            vbuf[op, i] = value
            gbuf[op, r] = value
        each_prod(lambda s: ag_copy(s).start())

        def fold(x):
            return jnp.sum(x, axis=0, keepdims=True)

        along_row = fold(along_part) + fold(cor_part)
        sc_send[op] = jnp.where(row_id == 0, fold(norm_part), jnp.where(row_id == 1, along_row, 0.0))
        for s in range(1, nr):
            sc_copy(s).start()
        tally = sc_send[op]
        for s in range(1, nr):
            sc_copy(s).wait_recv()
            tally = tally + sc_buf[op, s]
        sd_send[op] = tally
        each_prod(lambda s: sd_copy(s).start())

        def lift(first, op=op, image=image):
            wide = jnp.concatenate([gbuf[op, first + i] for i in range(slab)], axis=1)
            out = apply_map(pt2_ref[...], wide)
            for i in range(slab):
                r = first + i
                image[r] = (image[r] + mask_ref[r] * rows_w[kidx_ref[r]]) + out[:, i * horizon : (i + 1) * horizon]

        lift(mp * slab)

        def take(s, op=op):
            ag_copy(s).wait_recv()
            lift(lax.rem(mp - s + np_, np_) * slab)

        each_prod(take)
        each_prod(lambda s: sd_copy(s).wait_recv())
        tally = lax.fori_loop(1, np_, lambda s, c, op=op: c + sd_buf[op, s], sd_send[op])
        norm = jnp.sum(tally[0:1], axis=1, keepdims=True)
        along = jnp.sum(tally[1:2], axis=1, keepdims=True)
        if op == 0:
            alpha = norm / along

            def update(r, c, alpha=alpha):
                res_ref[r] = r0_buf[r] - alpha * img0[r]
                return c

            lax.fori_loop(0, regions, update, 0)
            norm_was, alpha_was = norm, alpha
        else:
            ratio = norm / norm_was
            alpha = norm / (along - ratio * norm / alpha_was)

            def finish(r, c, alpha=alpha, ratio=ratio):
                start, residual = r0_buf[r], res_ref[r]
                x_ref[r] = alpha_was * start + alpha * (residual + ratio * start)
                res_ref[r] = residual - alpha * (img1[r] + ratio * img0[r])
                return c

            lax.fori_loop(0, regions, finish, 0)

        for s in range(1, nr):
            row_copy(s).wait_send()
            sc_copy(s).wait_send()
        each_prod(lambda s: rs_copy(s).wait_send())
        each_prod(lambda s: cor_copy(s).wait_send())
        each_prod(lambda s: ag_copy(s).wait_send())
        each_prod(lambda s: sd_copy(s).wait_send())

    for s in range(1, nr):
        w_copy(s).wait_send()
        uz_copy(s).wait_send()
    each_prod(lambda s: a_copy(s).wait_send())
    each_prod(lambda s: v_copy(s).wait_send())


def on_device(nr, np_, bottom, gi_pred, ac_pred, gc_pred, bottom_w, gi_w, ac_w, gc_w, area_table, item_table):
    f32 = jnp.float32
    regions, items, horizon = bottom.shape
    groups, slots = area_table.shape
    classes = item_table.shape[0]
    gs, cs = gi_pred.shape[0], ac_pred.shape[1]
    slab = regions // np_
    per_tile = 8 // cs
    every = regions * nr
    most = min(slots, every - groups + 1)
    shared = 1 + min(groups - 1, every - most - (groups - 1))
    mr, mp = lax.axis_index("reg"), lax.axis_index("prod")

    def member(table, first, count):
        ids = first + jnp.arange(count, dtype=jnp.int32)
        return jnp.any(table[:, :, None] == ids[None, None, :], axis=1)

    area = member(area_table, mr * regions, regions)
    item = member(item_table, mp * items, items)
    sizes = jnp.sum((area_table >= 0).astype(jnp.int32), axis=1)
    ids = jnp.arange(groups, dtype=jnp.int32)
    ahead = (sizes[None, :] > sizes[:, None]) | ((sizes[None, :] == sizes[:, None]) & (ids[None, :] < ids[:, None]))
    rank = jnp.sum(ahead.astype(jnp.int32), axis=1)
    par = jnp.sum(jnp.where(area, ids[:, None], 0), axis=0)
    place = jnp.sum(jnp.where(area, rank[:, None], 0), axis=0)
    mask = (place < shared).astype(f32)
    kidx = jnp.minimum(place, shared - 1)
    single = (area & (rank[:, None] >= shared)).astype(f32)
    chosen = (rank[:, None] == jnp.arange(shared, dtype=jnp.int32)[None, :]).astype(f32)
    rs = jnp.concatenate([single, chosen], axis=1)
    rs = jnp.pad(rs, ((0, LANES - groups), (0, LANES - rs.shape[1])))

    itemf = item.astype(jnp.bfloat16)
    p2 = jnp.concatenate([itemf, itemf], axis=1)
    pt2 = jnp.concatenate([itemf.T, itemf.T], axis=1)
    by_owner = itemf.T.reshape(items, np_, 1, cs)
    eye = jnp.eye(per_tile, dtype=jnp.bfloat16)
    e = (eye[:, None, None, :, None] * by_owner[None]).reshape(per_tile * items, np_ * 8)
    e2 = jnp.concatenate([e, e], axis=1)

    weights = jnp.concatenate([gi_w.T, gc_w.T], axis=0)
    lanes = jnp.arange(LANES, dtype=jnp.int32)
    spread = (lanes[None, :] == mr * gs + jnp.arange(gs, dtype=jnp.int32)[:, None])
    wt = jnp.sum(jnp.where(spread[None], weights[:, :, None], 0.0), axis=1)
    spot = lax.rem(mp, per_tile) * cs + jnp.arange(cs, dtype=jnp.int32)
    rowsel = jnp.arange(8, dtype=jnp.int32)[:, None] == spot[None, :]
    at = jnp.sum(jnp.where(rowsel[:, :, None], ac_w.T[None], 0.0), axis=1)
    at = jnp.pad(at, ((0, 0), (0, LANES - regions)))
    dt = jnp.pad(bottom_w.T, ((0, 0), (0, LANES - regions)))
    u = gi_w[:, :, None] * gi_pred
    z = gc_w[:, :, None] * gc_pred
    v = (ac_w[:, :, None] * ac_pred).reshape(regions // per_tile, 8, horizon)

    field = (regions, items, horizon)
    two = ITERATIONS
    V = pltpu.VMEM
    dma = pltpu.SemaphoreType.DMA
    smem = pl.BlockSpec(memory_space=pltpu.SMEM)
    vmem = pl.BlockSpec(memory_space=pltpu.VMEM)
    return pl.pallas_call(
        functools.partial(kernel, nr, np_, shared, per_tile),
        out_shape=(jax.ShapeDtypeStruct(field, f32), jax.ShapeDtypeStruct(field, f32)),
        in_specs=[smem] * 3 + [vmem] * 11,
        out_specs=(vmem, vmem),
        scratch_shapes=[
            V((nr,) + wt.shape, f32),
            V((np_, 8, LANES), f32),
            V((groups, items, horizon), f32),
            V((np_, regions // per_tile, 8, horizon), f32),
            V((gs, items, horizon), f32),
            V(field, f32),
            V((slab, classes, horizon), f32),
            V((shared, items, horizon), f32),
            V((shared, classes, horizon), f32),
            V(field, f32),
            V(field, f32),
            V(field, f32),
            V((two, np_, slab, classes, horizon), f32),
            V((two, np_, slab, classes, horizon), f32),
            V((slab, classes, horizon), f32),
            V((two, slab, classes, horizon), f32),
            V((two, regions, classes, horizon), f32),
            V((two, shared, items, horizon), f32),
            V((two, nr, shared, items, horizon), f32),
            V((shared, items, horizon), f32),
            V((two, shared, classes, horizon), f32),
            V((two, np_, shared, classes, horizon), f32),
            V((shared, classes, horizon), f32),
            V((two, 8, horizon), f32),
            V((two, nr, 8, horizon), f32),
            V((two, 8, horizon), f32),
            V((two, np_, 8, horizon), f32),
            dma((nr,)), dma((nr,)), dma((nr,)), dma((nr,)),
            dma((np_,)), dma((np_,)), dma((np_,)), dma((np_,)),
            dma((two, np_)), dma((two, np_)), dma((two, np_)), dma((two, np_)),
            dma((two, nr)), dma((two, nr)), dma((two, np_)), dma((two, np_)),
            dma((two, nr)), dma((two, nr)), dma((two, np_)), dma((two, np_)),
        ],
        compiler_params=pltpu.CompilerParams(
            collective_id=0, has_side_effects=True, vmem_limit_bytes=60 * 1024 * 1024),
    )(par, kidx, mask, bottom, dt, u, z, v, wt, at, rs, p2, pt2, e2)


def solution(mesh):
    return jax.shard_map(
        functools.partial(on_device, mesh.shape["reg"], mesh.shape["prod"]),
        mesh=mesh,
        in_specs=(
            P("reg", "prod", None),
            P("reg", "prod", None),
            P("reg", "prod", None),
            P("reg", None, None),
            P("reg", "prod"),
            P("reg", "prod"),
            P("reg", "prod"),
            P("reg", None),
            P(),
            P(),
        ),
        out_specs=(P("reg", "prod", None), P("reg", "prod", None)),
        check_vma=False,
    )
```

time: 498 us -> 101 us (0.20)
  waiting for transfers between devices: 254 us -> 0 us
  blocking collectives: 194 us -> 0 us
  Pallas kernels: 0 us -> 85.3 us
  between operations: 21.7 us -> 0.76 us
  matrix products: 15.5 us -> 0 us
  other arithmetic: 3.64 us -> 8.92 us
    psum x2 -> x0, waiting for transfers between devices: 253 us -> none  [operate(): whole = lax.psum(partial_corner, ('reg', 'prod'))]
    all_gather x6 -> x0, blocking collectives: 118 us -> none  [the longest x3 94.6 us: disaggregate_onto(): lax.all_gather(lower, 'prod', axis=0, tiled=True)]
    pallas_call x0 -> x1, Pallas kernels: none -> 85.3 us  [on_device(): pl.pallas_call(functools.partial(kernel, nr, np_, shared, per_tile), out_...]
    psum x2 -> x0, blocking collectives: 76 us -> none  [two_products(): lax.psum((jnp.sum(vector * vector), jnp.sum(vector * image)), ('reg', 'pr...]
    dot_general x15 -> x0, matrix products: 15.5 us -> none  [the longest x3 4.43 us: disaggregate_onto(): jnp.einsum('pr,pqh->rqh', block, lax.all_gather(upper, 'reg', axis=0, til...]
  transfers between devices with their start and end apart: 6 -> 0, of which waited for: 2 -> 0; matrix products, arithmetic and copies ran while one was open for 2% -> 0% of each run, Pallas kernels for 0% -> 0%
where the time goes in v1:
time: 101 us
  Pallas kernels  85.3 us (84%)
  other arithmetic  8.92 us (9%)
  local copies, waits for them, and re-layouts  5.78 us (6%)
    pallas_call x1, Pallas kernels, on_device(): pl.pallas_call(functools.partial(kernel, nr, np_, shared, per_tile), out_...  85.3 us
    unnamed x24, local copies, waits for them, and re-layouts  4.03 us

profile of v1, /device:TPU:0, one launch (start us, length us, event | category | flops | bytes accessed | tf_op | source)
XLA Modules:
  0.0 100.7 jit_solution(649300738377046112)
XLA Ops:
  0.8 0.5 copy-done.4
  1.4 0.1 convert_reduce_fusion.1
  1.5 0.2 convert_reduce_fusion
  1.7 0.7 compare_reduce_fusion
  2.4 0.7 compare_reduce_fusion.1
  3.1 0.6 select_reduce_fusion.2
  3.8 0.5 compare_convert_fusion.1.mask_ref
  4.3 0.5 broadcast_minimum_fusion.kidx_ref
  4.9 0.6 pad.15.at_ref
  5.6 0.7 add_convert_fusion.p2_ref
  6.3 0.1 copy.28
  6.5 0.6 copy-done.5
  7.3 0.7 pad_maximum_fusion.1.pt2_ref
  8.0 0.6 pad.14.dt_ref
  8.7 0.1 broadcast_multiply_fusion.3
  8.9 0.1 copy.31
  9.0 0.7 pad_maximum_fusion.e2_ref
  9.8 0.7 select_reduce_fusion.wt_ref
  10.5 0.7 broadcast_multiply_fusion.2
  11.3 0.6 pad_convert_fusion.rs_ref
  11.9 0.8 broadcast_multiply_fusion
  12.7 85.3 %shard_map.113 = (f32[32,32,128]{2,1,0:T(8,128)}, f32[32,32,128]{2,1,0:T(8,128)}) custom-call(s32[32]{0:T(128)} %get-tuple-element.3.par_ref, s32[32]{0:T(128)} %broadcast_minimum_fusion.kidx_ref, f32[32]{0:T(128)} %compare_convert_fusion.1.mask_ref, f32[32,32,128]{2,1,0:T(8,128)} %b_ref.1, f32[32,128]{1,0:T(8,128)} %pad.14.dt_ref, ...), custom_call_target="tpu_custom_call" | custom-call | tf_op jit(solution)/shard_map/pallas_call | solution.py:361
  98.0 1.9 %copy.35 = f32[32,32,128]{2,1,0:T(8,128)} copy(f32[32,32,128]{2,1,0:T(8,128)} %get-tuple-element.10) | data formatting | bytes 1048576
  100.0 0.8 copy.36
  (37 shorter events, 1.0 us)
Async XLA Ops:
  0.6 0.7 copy-start.4
  0.7 1.0 copy-start.7
  3.8 1.1 %copy-start.9 = (f32[32,4]{0,1:T(4,128)S(1)}, f32[32,4]{0,1:T(4,128)}, u32[]{:S(2)}) copy-start(f32[32,4]{0,1:T(4,128)} %param.16) | copy-start | bytes 1540
  6.4 0.7 copy-start.5
  6.4 0.7 copy-start.6
  7.2 0.8 copy-start.8
  9.0 1.5 %copy-start.3 = (f32[32,4,128]{2,1,0:T(4,128)S(1)}, f32[32,4,128]{2,1,0:T(4,128)}, u32[]{:S(2)}) copy-start(f32[32,4,128]{2,1,0:T(4,128)} %param.12) | copy-start | bytes 196612
  9.8 2.1 %copy-start.1 = (f32[8,32,128]{2,1,0:T(8,128)S(1)}, f32[8,32,128]{2,1,0:T(8,128)}, u32[]{:S(2)}) copy-start(f32[8,32,128]{2,1,0:T(8,128)} %param.13) | copy-start | bytes 393220
  9.8 2.1 %copy-start.2 = (f32[8,32,128]{2,1,0:T(8,128)S(1)}, f32[8,32,128]{2,1,0:T(8,128)}, u32[]{:S(2)}) copy-start(f32[8,32,128]{2,1,0:T(8,128)} %param.11) | copy-start | bytes 393220
  98.0 1.9 %copy-start = (f32[32,32,128]{2,1,0:T(8,128)S(1)}, f32[32,32,128]{2,1,0:T(8,128)}, u32[]{:S(2)}) copy-start(f32[32,32,128]{2,1,0:T(8,128)} %get-tuple-element.11) | copy-start | bytes 1572868

commit v2 on v1

--- a/solution.py
+++ b/solution.py
@@ -10,6 +10,23 @@
 MESH = pl.DeviceIdType.MESH
 ITERATIONS = 2
 LANES = 128
+
+
+def steps(lo, hi, f, c, block=8):
+    count = hi - lo
+    if count <= block:
+        for i in range(lo, hi):
+            c = f(i, c)
+        return c
+    if count % block:
+        return lax.fori_loop(lo, hi, f, c)
+
+    def several(i, c):
+        for j in range(block):
+            c = f(lo + i * block + j, c)
+        return c
+
+    return lax.fori_loop(0, count // block, several, c)
 
 
 def halves(x):
@@ -29,7 +46,7 @@
     x_ref, res_ref,
     wt_buf, at_buf, uz_buf, g0_buf, uz_send,
     db, wcol, wgi, wgc, r0_buf, img0, img1,
-    col_send, rs_buf, own, vbuf, gbuf, row_send, row_buf, rows_w, cor_send, cor_buf, zed,
+    col_send, rs_buf, own, vbuf, gbuf, row_send, row_buf, rows_w, cor_send, cor_half, cor_buf, zed,
     sc_send, sc_buf, sd_send, sd_buf,
     s_w, r_w, s_uz, r_uz, s_a, r_a, s_v, r_v,
     s_rs, r_rs, s_ag, r_ag, s_row, r_row, s_cor, r_cor, s_sc, r_sc, s_sd, r_sd,
@@ -54,6 +71,28 @@
             src_ref=src, dst_ref=dst, send_sem=ss, recv_sem=rr,
             device_id=to("prod", mp, np_, s), device_id_type=MESH)
 
+    half = np_ // 2
+    local = lax.rem(mp, half)
+    home = mp - local
+    other = lax.rem(mp + half, np_)
+
+    def mate(s):
+        return home + lax.rem(local + s, half)
+
+    def giver(s):
+        return home + lax.rem(local + half - s, half)
+
+    def across(i):
+        return lax.rem(i + half, np_)
+
+    def each_mate(f):
+        steps(1, half, lambda s, c: (f(s), c)[1], 0)
+
+    def copy_to(i, src, dst, ss, rr):
+        return pltpu.make_async_remote_copy(
+            src_ref=src, dst_ref=dst, send_sem=ss, recv_sem=rr,
+            device_id={"prod": i}, device_id_type=MESH)
+
     barrier = pltpu.get_barrier_semaphore()
     for s in range(1, nr):
         pl.semaphore_signal(barrier, inc=1, device_id=to("reg", mr, nr, s), device_id_type=MESH)
@@ -62,13 +101,13 @@
         pl.semaphore_signal(barrier, inc=1, device_id=to("prod", mp, np_, s), device_id_type=MESH)
         return c
 
-    lax.fori_loop(1, np_, greet, 0)
+    steps(1, np_, greet, 0)
     for g in range(gs):
         uz_send[g] = u_ref[g] + apply_map(pt2_ref[...], z_ref[g])
     pl.semaphore_wait(barrier, nr - 1 + np_ - 1)
 
     def each_prod(f):
-        lax.fori_loop(1, np_, lambda s, c: (f(s), c)[1], 0)
+        steps(1, np_, lambda s, c: (f(s), c)[1], 0)
 
     def w_copy(s):
         return reg_copy(wt_ref, wt_buf.at[s], s_w.at[s], r_w.at[s], s)
@@ -79,12 +118,19 @@
     def a_copy(s):
         return prod_copy(at_ref, at_buf.at[mp], s_a.at[s], r_a.at[s], s)
 
+    def v_cross():
+        return copy_to(other, v_ref, g0_buf.at[mp], s_v.at[0], r_v.at[0])
+
     def v_copy(s):
-        return prod_copy(v_ref, g0_buf.at[mp], s_v.at[s], r_v.at[s], s)
+        return copy_to(mate(s), v_ref, g0_buf.at[mp], s_v.at[s], r_v.at[s])
+
+    def v_pass(s):
+        return copy_to(mate(s), g0_buf.at[other], g0_buf.at[other], s_v.at[half + s], r_v.at[half + s])
 
     for s in range(1, nr):
         w_copy(s).start()
-    each_prod(lambda s: v_copy(s).start())
+    v_cross().start()
+    each_mate(lambda s: v_copy(s).start())
     for s in range(1, nr):
         uz_copy(s).start()
     each_prod(lambda s: a_copy(s).start())
@@ -93,6 +139,8 @@
     for g in range(gs):
         uz_buf[mr * gs + g] = uz_send[g]
     base = dt_ref[...]
+    v_cross().wait_recv()
+    each_mate(lambda s: v_pass(s).start())
     for r in range(regions):
         r0_buf[r] = jnp.broadcast_to(base[:, r : r + 1], (items, horizon)) * b_ref[r]
     total = wt_ref[...]
@@ -122,7 +170,8 @@
 
     for s in range(1, nr):
         uz_copy(s).wait_recv()
-    each_prod(lambda s: v_copy(s).wait_recv())
+    each_mate(lambda s: v_copy(s).wait_recv())
+    each_mate(lambda s: v_pass(s).wait_recv())
 
     def first_field(a, c):
         flat = jnp.concatenate([g0_buf[j, a] for j in range(np_)], axis=0)
@@ -132,7 +181,7 @@
             r0_buf[r] = r0_buf[r] + uz_buf[par_ref[r]] + lifted[t * items : (t + 1) * items]
         return c
 
-    lax.fori_loop(0, regions // per_tile, first_field, 0)
+    steps(0, regions // per_tile, first_field, 0)
 
     row_id = lax.broadcasted_iota(jnp.int32, (8, horizon), 0)
     norm_was = alpha_was = None
@@ -143,14 +192,30 @@
         def row_copy(s, op=op):
             return reg_copy(row_send.at[op], row_buf.at[op, s], s_row.at[op, s], r_row.at[op, s], s)
 
-        def rs_copy(s, op=op):
-            return prod_copy(col_send.at[op, s], rs_buf.at[op, s], s_rs.at[op, s], r_rs.at[op, s], s)
+        def rs_copy(s, slot, op=op):
+            return copy_to(mate(s), col_send.at[op, slot], rs_buf.at[op, slot], s_rs.at[op, slot], r_rs.at[op, slot])
+
+        def rs_cross(op=op):
+            return copy_to(other, col_send.at[op, 0], rs_buf.at[op, 0], s_rs.at[op, 0], r_rs.at[op, 0])
 
         def cor_copy(s, op=op):
-            return prod_copy(cor_send.at[op], cor_buf.at[op, s], s_cor.at[op, s], r_cor.at[op, s], s)
+            return copy_to(mate(s), cor_send.at[op], cor_buf.at[op, s], s_cor.at[op, s], r_cor.at[op, s])
+
+        def cor_cross(op=op):
+            return copy_to(other, cor_half.at[op], cor_buf.at[op, 0], s_cor.at[op, 0], r_cor.at[op, 0])
+
+        def mine(i):
+            return pl.ds(i * slab, slab)
 
         def ag_copy(s, op=op):
-            return prod_copy(vbuf.at[op], gbuf.at[op, pl.ds(mp * slab, slab)], s_ag.at[op, s], r_ag.at[op, s], s)
+            return copy_to(mate(s), vbuf.at[op], gbuf.at[op, mine(mp)], s_ag.at[op, s], r_ag.at[op, s])
+
+        def ag_cross(op=op):
+            return copy_to(other, vbuf.at[op], gbuf.at[op, mine(mp)], s_ag.at[op, 0], r_ag.at[op, 0])
+
+        def ag_pass(s, op=op):
+            block = gbuf.at[op, mine(other)]
+            return copy_to(mate(s), block, block, s_ag.at[op, half + s], r_ag.at[op, half + s])
 
         def sc_copy(s, op=op):
             return reg_copy(sc_send.at[op], sc_buf.at[op, s], s_sc.at[op, s], r_sc.at[op, s], s)
@@ -162,27 +227,29 @@
             def add(r, acc):
                 return acc + jnp.where(kidx_ref[r] == k, mask_ref[r], 0.0) * field[r]
 
-            row_send[op, k] = lax.fori_loop(0, regions, add, jnp.zeros((items, horizon), jnp.float32))
+            row_send[op, k] = steps(0, regions, add, jnp.zeros((items, horizon), jnp.float32), 32)
             return c
 
-        lax.fori_loop(0, shared, one_row, 0)
+        steps(0, shared, one_row, 0)
         for s in range(1, nr):
             row_copy(s).start()
 
-        def columns(s, op=op, field=field):
-            first = lax.rem(mp + s, np_) * slab
+        def columns(i, field=field):
+            first = i * slab
             wide = jnp.concatenate([field[first + i] for i in range(slab)], axis=1)
             out = apply_map(p2_ref[...], wide)
             return [out[:, i * horizon : (i + 1) * horizon] for i in range(slab)]
 
-        def send_columns(s, op=op):
-            for i, one in enumerate(columns(s)):
-                col_send[op, s, i] = one
-            rs_copy(s).start()
-
-        each_prod(send_columns)
-        for i, one in enumerate(columns(0)):
+        def send_columns(s, slot, owner, op=op):
+            for i, one in enumerate(columns(owner)):
+                col_send[op, slot, i] = one
+            rs_copy(s, slot).start()
+
+        each_mate(lambda s: send_columns(s, half + s, across(mate(s))))
+        each_mate(lambda s: send_columns(s, s, mate(s)))
+        for i, one in enumerate(columns(mp)):
             own[i] = one
+        theirs = columns(other)
 
         for s in range(1, nr):
             row_copy(s).wait_recv()
@@ -196,8 +263,22 @@
             cor_send[op, k] = apply_map(p2_ref[...], rows)
             return acc + weighted * rows
 
-        row_part = lax.fori_loop(0, shared, one_corner, jnp.zeros((items, horizon), jnp.float32))
-        each_prod(lambda s: cor_copy(s).start())
+        row_part = steps(0, shared, one_corner, jnp.zeros((items, horizon), jnp.float32))
+        each_mate(lambda s: cor_copy(s).start())
+
+        each_mate(lambda s: rs_copy(s, half + s).wait_recv())
+        for i in range(slab):
+            col_send[op, 0, i] = steps(1, half, lambda s, c, i=i, op=op: c + rs_buf[op, half + s, i], theirs[i])
+        rs_cross().start()
+
+        each_mate(lambda s: cor_copy(s).wait_recv())
+
+        def half_corner(k, c, op=op):
+            cor_half[op, k] = steps(1, half, lambda s, t: t + cor_buf[op, s, k], cor_send[op, k])
+            return c
+
+        steps(0, shared, half_corner, 0)
+        cor_cross().start()
 
         def diagonal(r, acc, field=field, image=image):
             v = field[r]
@@ -206,30 +287,32 @@
             return acc[0] + v * v, acc[1] + w * v
 
         zero = jnp.zeros((items, horizon), jnp.float32)
-        norm_part, along_part = lax.fori_loop(0, regions, diagonal, (zero, zero))
+        norm_part, along_part = steps(0, regions, diagonal, (zero, zero))
         along_part = along_part + row_part * (1.0 / nr)
 
-        each_prod(lambda s: cor_copy(s).wait_recv())
+        cor_cross().wait_recv()
 
         def one_zed(k, acc, op=op):
-            corner = lax.fori_loop(1, np_, lambda s, c: c + cor_buf[op, s, k], cor_send[op, k])
+            corner = cor_half[op, k] + cor_buf[op, 0, k]
             weighted = wgc[k] * corner
             zed[k] = weighted
             return acc + weighted * corner
 
         czero = jnp.zeros((classes, horizon), jnp.float32)
-        cor_part = lax.fori_loop(0, shared, one_zed, czero) * (1.0 / (nr * np_))
-
-        each_prod(lambda s: rs_copy(s).wait_recv())
+        cor_part = steps(0, shared, one_zed, czero) * (1.0 / (nr * np_))
+
+        each_mate(lambda s: rs_copy(s, s).wait_recv())
+        rs_cross().wait_recv()
         for i in range(slab):
             r = mp * slab + i
-            cols = lax.fori_loop(1, np_, lambda s, c, i=i, op=op: c + rs_buf[op, s, i], own[i])
+            cols = steps(0, half, lambda s, c, i=i, op=op: c + rs_buf[op, s, i], own[i])
             weighted = wcol[i] * cols
             cor_part = cor_part + weighted * cols
             value = weighted + mask_ref[r] * zed[kidx_ref[r]]
             vbuf[op, i] = value
             gbuf[op, r] = value
-        each_prod(lambda s: ag_copy(s).start())
+        ag_cross().start()
+        each_mate(lambda s: ag_copy(s).start())
 
         def fold(x):
             return jnp.sum(x, axis=0, keepdims=True)
@@ -238,6 +321,8 @@
         sc_send[op] = jnp.where(row_id == 0, fold(norm_part), jnp.where(row_id == 1, along_row, 0.0))
         for s in range(1, nr):
             sc_copy(s).start()
+        ag_cross().wait_recv()
+        each_mate(lambda s: ag_pass(s).start())
         tally = sc_send[op]
         for s in range(1, nr):
             sc_copy(s).wait_recv()
@@ -253,14 +338,20 @@
                 image[r] = (image[r] + mask_ref[r] * rows_w[kidx_ref[r]]) + out[:, i * horizon : (i + 1) * horizon]
 
         lift(mp * slab)
-
-        def take(s, op=op):
+        lift(other * slab)
+
+        def take(s):
             ag_copy(s).wait_recv()
-            lift(lax.rem(mp - s + np_, np_) * slab)
-
-        each_prod(take)
+            lift(giver(s) * slab)
+
+        def take_passed(s):
+            ag_pass(s).wait_recv()
+            lift(across(giver(s)) * slab)
+
+        each_mate(take)
+        each_mate(take_passed)
         each_prod(lambda s: sd_copy(s).wait_recv())
-        tally = lax.fori_loop(1, np_, lambda s, c, op=op: c + sd_buf[op, s], sd_send[op])
+        tally = steps(1, np_, lambda s, c, op=op: c + sd_buf[op, s], sd_send[op])
         norm = jnp.sum(tally[0:1], axis=1, keepdims=True)
         along = jnp.sum(tally[1:2], axis=1, keepdims=True)
         if op == 0:
@@ -270,7 +361,7 @@
                 res_ref[r] = r0_buf[r] - alpha * img0[r]
                 return c
 
-            lax.fori_loop(0, regions, update, 0)
+            steps(0, regions, update, 0)
             norm_was, alpha_was = norm, alpha
         else:
             ratio = norm / norm_was
@@ -282,21 +373,28 @@
                 res_ref[r] = residual - alpha * (img1[r] + ratio * img0[r])
                 return c
 
-            lax.fori_loop(0, regions, finish, 0)
+            steps(0, regions, finish, 0)
 
         for s in range(1, nr):
             row_copy(s).wait_send()
             sc_copy(s).wait_send()
-        each_prod(lambda s: rs_copy(s).wait_send())
-        each_prod(lambda s: cor_copy(s).wait_send())
-        each_prod(lambda s: ag_copy(s).wait_send())
+        each_mate(lambda s: rs_copy(s, s).wait_send())
+        each_mate(lambda s: rs_copy(s, half + s).wait_send())
+        each_mate(lambda s: cor_copy(s).wait_send())
+        each_mate(lambda s: ag_copy(s).wait_send())
+        each_mate(lambda s: ag_pass(s).wait_send())
+        rs_cross().wait_send()
+        cor_cross().wait_send()
+        ag_cross().wait_send()
         each_prod(lambda s: sd_copy(s).wait_send())
 
     for s in range(1, nr):
         w_copy(s).wait_send()
         uz_copy(s).wait_send()
     each_prod(lambda s: a_copy(s).wait_send())
-    each_prod(lambda s: v_copy(s).wait_send())
+    v_cross().wait_send()
+    each_mate(lambda s: v_copy(s).wait_send())
+    each_mate(lambda s: v_pass(s).wait_send())
 
 
 def on_device(nr, np_, bottom, gi_pred, ac_pred, gc_pred, bottom_w, gi_w, ac_w, gc_w, area_table, item_table):
@@ -305,7 +403,7 @@
     groups, slots = area_table.shape
     classes = item_table.shape[0]
     gs, cs = gi_pred.shape[0], ac_pred.shape[1]
-    slab = regions // np_
+    slab, half = regions // np_, np_ // 2
     per_tile = 8 // cs
     every = regions * nr
     most = min(slots, every - groups + 1)
@@ -385,7 +483,8 @@
             V((two, nr, shared, items, horizon), f32),
             V((shared, items, horizon), f32),
             V((two, shared, classes, horizon), f32),
-            V((two, np_, shared, classes, horizon), f32),
+            V((two, shared, classes, horizon), f32),
+            V((two, half, shared, classes, horizon), f32),
             V((shared, classes, horizon), f32),
             V((two, 8, horizon), f32),
             V((two, nr, 8, horizon), f32),
@@ -394,7 +493,7 @@
             dma((nr,)), dma((nr,)), dma((nr,)), dma((nr,)),
             dma((np_,)), dma((np_,)), dma((np_,)), dma((np_,)),
             dma((two, np_)), dma((two, np_)), dma((two, np_)), dma((two, np_)),
-            dma((two, nr)), dma((two, nr)), dma((two, np_)), dma((two, np_)),
+            dma((two, nr)), dma((two, nr)), dma((two, half)), dma((two, half)),
             dma((two, nr)), dma((two, nr)), dma((two, np_)), dma((two, np_)),
         ],
         compiler_params=pltpu.CompilerParams(

time: 101 us -> 78.2 us (0.77)
  Pallas kernels: 85.3 us -> 62.3 us
    pallas_call x1, Pallas kernels: 85.3 us -> 62.3 us  [on_device(): pl.pallas_call(functools.partial(kernel, nr, np_, shared, per_tile), out_...]
where the time goes in v2:
time: 78.2 us; the launch traced here: 77.8 us
  Pallas kernels  62.3 us (80%)
  other arithmetic  8.92 us (11%)
  local copies, waits for them, and re-layouts  5.78 us (7%)
    pallas_call x1, Pallas kernels, on_device(): pl.pallas_call(functools.partial(kernel, nr, np_, shared, per_tile), out_...  62.3 us
    unnamed x24, local copies, waits for them, and re-layouts  4.03 us

profile of v2, /device:TPU:0, one launch (start us, length us, event | category | flops | bytes accessed | tf_op | source)
XLA Modules:
  0.0 77.8 jit_solution(14853179033147547211)
XLA Ops:
  0.8 0.5 copy-done.4
  1.4 0.1 convert_reduce_fusion.1
  1.5 0.2 convert_reduce_fusion
  1.7 0.7 compare_reduce_fusion
  2.4 0.7 compare_reduce_fusion.1
  3.1 0.6 select_reduce_fusion.2
  3.8 0.5 compare_convert_fusion.1.mask_ref
  4.3 0.5 broadcast_minimum_fusion.kidx_ref
  4.9 0.6 pad.15.at_ref
  5.6 0.7 add_convert_fusion.p2_ref
  6.3 0.1 copy.28
  6.5 0.6 copy-done.5
  7.3 0.7 pad_maximum_fusion.1.pt2_ref
  8.0 0.6 pad.14.dt_ref
  8.7 0.1 broadcast_multiply_fusion.3
  8.9 0.1 copy.31
  9.0 0.7 pad_maximum_fusion.e2_ref
  9.8 0.7 select_reduce_fusion.wt_ref
  10.5 0.7 broadcast_multiply_fusion.2
  11.3 0.6 pad_convert_fusion.rs_ref
  11.9 0.8 %broadcast_multiply_fusion = (f32[8,32,128]{2,1,0:T(8,128)}, f32[8,32,128]{2,1,0:T(8,128)}) fusion(f32[8,32,128]{2,1,0:T(8,128)S(1)} %copy-done.1, f32[8,32]{1,0:T(8,128)S(1)} %copy-done.5, f32[8,32,128]{2,1,0:T(8,128)S(1)} %copy-done.2, f32[8,32]{1,0:T(8,128)S(1)} %copy-done.6), kind=kLoop, calls=%fused_computation.3 | loop fusion | flops 65536 | bytes 526336 | tf_op jit(solution)/shard_map/mul | solution.py:450
  12.7 62.3 %shard_map.113 = (f32[32,32,128]{2,1,0:T(8,128)}, f32[32,32,128]{2,1,0:T(8,128)}) custom-call(s32[32]{0:T(128)} %get-tuple-element.3.par_ref, s32[32]{0:T(128)} %broadcast_minimum_fusion.kidx_ref, f32[32]{0:T(128)} %compare_convert_fusion.1.mask_ref, f32[32,32,128]{2,1,0:T(8,128)} %b_ref.1, f32[32,128]{1,0:T(8,128)} %pad.14.dt_ref, ...), custom_call_target="tpu_custom_call" | custom-call | tf_op jit(solution)/shard_map/pallas_call | solution.py:459
  75.1 1.9 %copy.35 = f32[32,32,128]{2,1,0:T(8,128)} copy(f32[32,32,128]{2,1,0:T(8,128)} %get-tuple-element.10) | data formatting | bytes 1048576
  77.0 0.8 %copy.36 = f32[32,32,128]{2,1,0:T(8,128)} copy(f32[32,32,128]{2,1,0:T(8,128)S(1)} %copy-done) | data formatting | bytes 1048576
  (37 shorter events, 1.0 us)
Async XLA Ops:
  0.6 0.7 copy-start.4
  0.7 1.0 %copy-start.7 = (s32[32,128]{1,0:T(8,128)S(1)}, s32[32,128]{1,0:T(8,128)}, u32[]{:S(2)}) copy-start(s32[32,128]{1,0:T(8,128)} %param.19) | copy-start | bytes 49156
  3.8 1.1 %copy-start.9 = (f32[32,4]{0,1:T(4,128)S(1)}, f32[32,4]{0,1:T(4,128)}, u32[]{:S(2)}) copy-start(f32[32,4]{0,1:T(4,128)} %param.16) | copy-start | bytes 1540
  6.4 0.7 copy-start.5
  6.4 0.7 copy-start.6
  7.2 0.8 copy-start.8
  9.0 1.5 %copy-start.3 = (f32[32,4,128]{2,1,0:T(4,128)S(1)}, f32[32,4,128]{2,1,0:T(4,128)}, u32[]{:S(2)}) copy-start(f32[32,4,128]{2,1,0:T(4,128)} %param.12) | copy-start | bytes 196612
  9.8 2.1 %copy-start.1 = (f32[8,32,128]{2,1,0:T(8,128)S(1)}, f32[8,32,128]{2,1,0:T(8,128)}, u32[]{:S(2)}) copy-start(f32[8,32,128]{2,1,0:T(8,128)} %param.13) | copy-start | bytes 393220
  9.8 2.1 %copy-start.2 = (f32[8,32,128]{2,1,0:T(8,128)S(1)}, f32[8,32,128]{2,1,0:T(8,128)}, u32[]{:S(2)}) copy-start(f32[8,32,128]{2,1,0:T(8,128)} %param.11) | copy-start | bytes 393220
  75.0 1.9 %copy-start = (f32[32,32,128]{2,1,0:T(8,128)S(1)}, f32[32,32,128]{2,1,0:T(8,128)}, u32[]{:S(2)}) copy-start(f32[32,32,128]{2,1,0:T(8,128)} %get-tuple-element.11) | copy-start | bytes 1572868

commit v3 on v2

--- a/solution.py
+++ b/solution.py
@@ -130,10 +130,10 @@
     for s in range(1, nr):
         w_copy(s).start()
     v_cross().start()
+    each_prod(lambda s: a_copy(s).start())
     each_mate(lambda s: v_copy(s).start())
     for s in range(1, nr):
         uz_copy(s).start()
-    each_prod(lambda s: a_copy(s).start())
     g0_buf[mp] = v_ref[...]
     at_buf[mp] = at_ref[...]
     for g in range(gs):
@@ -321,14 +321,14 @@
         sc_send[op] = jnp.where(row_id == 0, fold(norm_part), jnp.where(row_id == 1, along_row, 0.0))
         for s in range(1, nr):
             sc_copy(s).start()
-        ag_cross().wait_recv()
-        each_mate(lambda s: ag_pass(s).start())
         tally = sc_send[op]
         for s in range(1, nr):
             sc_copy(s).wait_recv()
             tally = tally + sc_buf[op, s]
         sd_send[op] = tally
         each_prod(lambda s: sd_copy(s).start())
+        ag_cross().wait_recv()
+        each_mate(lambda s: ag_pass(s).start())
 
         def lift(first, op=op, image=image):
             wide = jnp.concatenate([gbuf[op, first + i] for i in range(slab)], axis=1)

time: 78.2 us -> 77.7 us (level)
  no operation moved by 1% of the time
where the time goes in v3:
time: 77.7 us; the launch traced here: 77.3 us
  Pallas kernels  61.9 us (80%)
  other arithmetic  8.92 us (11%)
  local copies, waits for them, and re-layouts  5.78 us (7%)
    pallas_call x1, Pallas kernels, on_device(): pl.pallas_call(functools.partial(kernel, nr, np_, shared, per_tile), out_...  61.9 us
    unnamed x24, local copies, waits for them, and re-layouts  4.03 us

profile of v3, /device:TPU:0, one launch (start us, length us, event | category | flops | bytes accessed | tf_op | source)
XLA Modules:
  0.0 77.3 jit_solution(13756578959537930159)
XLA Ops:
  0.8 0.5 copy-done.4
  1.4 0.1 convert_reduce_fusion.1
  1.5 0.2 convert_reduce_fusion
  1.7 0.7 compare_reduce_fusion
  2.4 0.7 compare_reduce_fusion.1
  3.1 0.6 select_reduce_fusion.2
  3.8 0.5 compare_convert_fusion.1.mask_ref
  4.3 0.5 broadcast_minimum_fusion.kidx_ref
  4.9 0.6 pad.15.at_ref
  5.6 0.7 add_convert_fusion.p2_ref
  6.3 0.1 copy.28
  6.5 0.6 copy-done.5
  7.3 0.7 pad_maximum_fusion.1.pt2_ref
  8.0 0.6 pad.14.dt_ref
  8.7 0.1 broadcast_multiply_fusion.3
  8.9 0.1 copy.31
  9.0 0.7 pad_maximum_fusion.e2_ref
  9.8 0.7 select_reduce_fusion.wt_ref
  10.5 0.7 broadcast_multiply_fusion.2
  11.3 0.6 pad_convert_fusion.rs_ref
  11.9 0.8 %broadcast_multiply_fusion = (f32[8,32,128]{2,1,0:T(8,128)}, f32[8,32,128]{2,1,0:T(8,128)}) fusion(f32[8,32,128]{2,1,0:T(8,128)S(1)} %copy-done.1, f32[8,32]{1,0:T(8,128)S(1)} %copy-done.5, f32[8,32,128]{2,1,0:T(8,128)S(1)} %copy-done.2, f32[8,32]{1,0:T(8,128)S(1)} %copy-done.6), kind=kLoop, calls=%fused_computation.3 | loop fusion | flops 65536 | bytes 526336 | tf_op jit(solution)/shard_map/mul | solution.py:450
  12.7 61.9 %shard_map.113 = (f32[32,32,128]{2,1,0:T(8,128)}, f32[32,32,128]{2,1,0:T(8,128)}) custom-call(s32[32]{0:T(128)} %get-tuple-element.3.par_ref, s32[32]{0:T(128)} %broadcast_minimum_fusion.kidx_ref, f32[32]{0:T(128)} %compare_convert_fusion.1.mask_ref, f32[32,32,128]{2,1,0:T(8,128)} %b_ref.1, f32[32,128]{1,0:T(8,128)} %pad.14.dt_ref, ...), custom_call_target="tpu_custom_call" | custom-call | tf_op jit(solution)/shard_map/pallas_call | solution.py:459
  74.6 1.9 %copy.35 = f32[32,32,128]{2,1,0:T(8,128)} copy(f32[32,32,128]{2,1,0:T(8,128)} %get-tuple-element.10) | data formatting | bytes 1048576
  76.5 0.8 %copy.36 = f32[32,32,128]{2,1,0:T(8,128)} copy(f32[32,32,128]{2,1,0:T(8,128)S(1)} %copy-done) | data formatting | bytes 1048576
  (37 shorter events, 1.0 us)
Async XLA Ops:
  0.6 0.7 copy-start.4
  0.7 1.0 %copy-start.7 = (s32[32,128]{1,0:T(8,128)S(1)}, s32[32,128]{1,0:T(8,128)}, u32[]{:S(2)}) copy-start(s32[32,128]{1,0:T(8,128)} %param.19) | copy-start | bytes 49156
  3.8 1.1 %copy-start.9 = (f32[32,4]{0,1:T(4,128)S(1)}, f32[32,4]{0,1:T(4,128)}, u32[]{:S(2)}) copy-start(f32[32,4]{0,1:T(4,128)} %param.16) | copy-start | bytes 1540
  6.4 0.7 copy-start.5
  6.4 0.7 copy-start.6
  7.2 0.8 copy-start.8
  9.0 1.5 %copy-start.3 = (f32[32,4,128]{2,1,0:T(4,128)S(1)}, f32[32,4,128]{2,1,0:T(4,128)}, u32[]{:S(2)}) copy-start(f32[32,4,128]{2,1,0:T(4,128)} %param.12) | copy-start | bytes 196612
  9.8 2.1 %copy-start.1 = (f32[8,32,128]{2,1,0:T(8,128)S(1)}, f32[8,32,128]{2,1,0:T(8,128)}, u32[]{:S(2)}) copy-start(f32[8,32,128]{2,1,0:T(8,128)} %param.13) | copy-start | bytes 393220
  9.8 2.1 %copy-start.2 = (f32[8,32,128]{2,1,0:T(8,128)S(1)}, f32[8,32,128]{2,1,0:T(8,128)}, u32[]{:S(2)}) copy-start(f32[8,32,128]{2,1,0:T(8,128)} %param.11) | copy-start | bytes 393220
  74.6 1.9 %copy-start = (f32[32,32,128]{2,1,0:T(8,128)S(1)}, f32[32,32,128]{2,1,0:T(8,128)}, u32[]{:S(2)}) copy-start(f32[32,32,128]{2,1,0:T(8,128)} %get-tuple-element.11) | copy-start | bytes 1572868
